TPU v7x, 32 devices: a whole 2x2x4 slice. The times are simulated.
32 devices in a mesh: pole: 4 (over y, core), dom: 8 (over z, x).
Axes of the slice: x: 2, y: 2, z: 4, core: 2. Of those that a mesh axis runs over, the one named last changes fastest.
Arguments:
- initial_block: bfloat16 [8, 8, 512, 256], P('dom'), may hold values from -24 to 24
- coupling: bfloat16 [8, 8, 512, 512], P('dom'), may hold values from -0.125 to 0.125
- pivots: bfloat16 [4, 8, 8, 2, 512, 512], P('pole', 'dom'), may hold values from -0.125 to 0.125
- interface: bfloat16 [4, 8, 3, 2, 512, 512], P('pole', 'dom'), may hold values from -0.1875 to 0.1875
- pole_values: float32 [4, 4], P('pole'), may hold values from 0.5 to 1.5
Outputs:
- filtered_basis: float32 [8, 8, 512, 256], P('dom', 'pole')
- rayleigh: float32 [256, 256], replicated
All inputs are finite; a program needn't handle non-finite values.
Results may differ from a plain program's by a relative error of at most 0.008.
Values sent between devices are 32-bit elements; how exact they have to be, the bound alone decides.
No kernel may reach another device: no remote copies, remote signals or barrier semaphores. Data moves between devices by JAX's collectives and lax.ppermute only.
A program may use at most 192 MiB of HBM per device.

v0:
```python
import jax
import jax.numpy as jnp
from jax import lax
from jax.sharding import PartitionSpec as P

B = 512
M = 256


def shifted(x, axis, by):
    length = lax.axis_size(axis)
    pairs = [(i, i + by) for i in range(length) if 0 <= i + by < length]
    return lax.ppermute(x, axis, pairs)


def lower_solve(factor, right_side):
    return lax.linalg.triangular_solve(factor, right_side, left_side=True, lower=True)


def complex_product(matrix, vectors):
    block_order = matrix.shape[1]
    half_width = vectors.shape[1] // 2
    stacked = matrix.reshape(2 * block_order, block_order)
    stacked_out = jnp.dot(stacked, vectors.astype(jnp.bfloat16), preferred_element_type=jnp.float32)
    real_part = stacked_out[:block_order, :half_width] - stacked_out[block_order:, half_width:]
    imag_part = stacked_out[:block_order, half_width:] + stacked_out[block_order:, :half_width]
    return jnp.concatenate([real_part, imag_part], axis=1)


def real_product(matrix, vectors):
    return jnp.dot(matrix, vectors.astype(jnp.bfloat16), preferred_element_type=jnp.float32)


def transposed_product(matrix, vectors):
    return lax.dot_general(
        matrix,
        vectors.astype(jnp.bfloat16),
        (((0,), (0,)), ((), ())),
        preferred_element_type=jnp.float32,
    )


def inner_products(left, right_side):
    return lax.dot_general(
        left,
        right_side,
        (((0,), (0,)), ((), ())),
        precision=lax.Precision.HIGHEST,
        preferred_element_type=jnp.float32,
    )


def partition_solve(inverse, coupled, source):
    previous = jnp.roll(coupled, 1, axis=0)
    initial = jnp.zeros(source.shape[1:], jnp.float32)

    def forward_step(carried, members):
        block_inverse, given, couple_prev = members
        result = complex_product(block_inverse, given + transposed_product(couple_prev, carried))
        return (result, result)

    unused, forward = lax.scan(forward_step, initial, (inverse, source, previous))

    def backward_step(carried, members):
        block_inverse, partial_value, couple_next = members
        result = partial_value + complex_product(block_inverse, real_product(couple_next, carried))
        return (result, result)

    unused, backward = lax.scan(backward_step, initial, (inverse, forward, coupled), reverse=True)
    return backward


def on_device(initial_block, coupling, pivots, interface, pole_values):
    blocks = coupling.shape[1]
    coupled = coupling[0]
    inverse = pivots[0, 0]
    factors = interface[0, 0]
    real_start = initial_block[0].astype(jnp.float32)
    source = jnp.concatenate([real_start, jnp.zeros_like(real_start)], axis=-1)
    first = partition_solve(inverse, coupled, source)
    bottom = first[blocks - 1]
    top = first[0]
    top_next = shifted(top, "dom", -1)
    below = complex_product(factors[0], bottom) - complex_product(factors[1], top_next)
    topmost = lax.axis_index("dom") == lax.axis_size("dom") - 1
    above = jnp.where(
        topmost, jnp.zeros_like(top_next), top_next - complex_product(factors[2], below)
    )
    link = coupled[blocks - 1]
    lifted = transposed_product(link, below)
    arriving = shifted(lifted, "dom", 1)
    update = source.at[0].add(arriving)
    update = update.at[blocks - 1].add(real_product(link, above))
    second = partition_solve(inverse, coupled, update)
    real_z = pole_values[0, 0]
    imag_z = pole_values[0, 1]
    real_w = pole_values[0, 2]
    imag_w = pole_values[0, 3]
    real_x = second[..., :M]
    imag_x = second[..., M:]
    filtered_term = real_w * real_x - imag_w * imag_x
    shifted_term = (
        (real_w * real_z - imag_w * imag_z) * real_x
        - (real_w * imag_z + imag_w * real_z) * imag_x
        - real_w * real_start
    )
    count = blocks // lax.axis_size("pole")
    summed = lax.psum(filtered_term, "pole")
    offset = lax.axis_index("pole") * count
    own_rows = lax.dynamic_slice_in_dim(summed, offset, count, 0).reshape(count * B, M)
    gram_part = inner_products(own_rows, own_rows)
    projected_part = inner_products(
        summed.reshape(blocks * B, M), shifted_term.reshape(blocks * B, M)
    )
    gram_total, projected_total = lax.psum((gram_part, projected_part), ("pole", "dom"))
    row_total = blocks * B * lax.axis_size("dom")
    gram = gram_total / row_total
    projected = projected_total / row_total
    factor = jnp.linalg.cholesky(gram)
    filtered_basis = lower_solve(factor, own_rows.T).T.reshape(1, count, B, M)
    middle = lower_solve(factor, projected)
    rayleigh = lower_solve(factor, middle.T).T
    return (filtered_basis, rayleigh)


def solution(mesh):
    in_specs = (
        P("dom", None, None, None),
        P("dom", None, None, None),
        P("pole", "dom", None, None, None, None),
        P("pole", "dom", None, None, None, None),
        P("pole", None),
    )
    out_specs = (P("dom", "pole", None, None), P())
    return jax.shard_map(
        on_device, mesh=mesh, in_specs=in_specs, out_specs=out_specs, check_vma=False
    )
```

profile of v0, /device:TPU:0, one launch (start us, length us, event | category | flops | bytes accessed | tf_op | source)
XLA Modules:
  0.0 687.2 jit_solution(11109018124211285651)
XLA Ops:
  7.2 4.2 slice_bitcast_fusion
  12.5 2.9 copy.17
  18.0 4.2 concatenate.76
  24.6 4.3 broadcast.158.clone.2
  29.7 65.2 %while.65 = (s32[]{:T(128)}, bf16[512,512]{0,1:T(8,128)(2,1)}, f32[8,512,512]{1,2,0:T(8,128)}, bf16[8,2,512,512]{3,2,1,0:T(8,128)(2,1)}, f32[8,512,512]{1,2,0:T(8,128)}, /*index=5*/bf16[8,512,512]{2,1,0:T(8,128)(2,1)}, s32[]{:T(128)}) while((s32[]{:T(128)}, bf16[512,512]{0,1:T(8,128)(2,1)}, f32[8,512,512]{1,2,0:T(8,128)}, ...), condition=%wide.region_1.2_spmd, body=%wide.region_0.1_spmd.sunk | while | flops 806617088 | bytes 17302612 | solution.py:62
  33.6 2.7 fusion.145
  41.8 2.7 fusion.145
  50.0 2.7 fusion.145
  58.1 2.7 fusion.145
  66.3 2.7 fusion.145
  74.5 2.7 fusion.145
  82.6 2.7 fusion.145
  90.7 2.7 fusion.145
  95.0 4.3 broadcast.158.clone.1
  99.3 67.7 %while.68 = (s32[]{:T(128)}, bf16[512,512]{0,1:T(8,128)(2,1)}, f32[8,512,512]{1,2,0:T(8,128)}, f32[8,512,512]{1,2,0:T(8,128)}, bf16[8,2,512,512]{3,2,1,0:T(8,128...) while((s32[]{:T(128)}, bf16[512,512]{0,1:T(8,128)(2,1)}, ...), condition=%wide.region_3.4_spmd.clone, body=%wide.region_2.3_spmd.clone.sunk | while | flops 807403520 | bytes 15204483 | solution.py:69
  103.0 2.5 fusion.154
  120.0 2.4 fusion.154
  136.9 2.4 fusion.154
  173.8 22.5 %collective-permute-done = f32[512,512]{0,1:T(8,128)S(1)} collective-permute-done((f32[512,512]{0,1:T(8,128)S(1)}, f32[512,512]{0,1:T(8,128)S(1)}, u32[]{:S(2)}, u32[]{:S(2)}) %collective-permute-start) | collective-permute-done | bytes 1048608 | tf_op jit(solution)/shard_map/ppermute | solution.py:13
  197.6 2.5 convolution_bitcast_fusion.4
  200.0 6.1 collective-permute-start.1
  207.7 18.7 %collective-permute-done.1 = f32[512,512]{0,1:T(8,128)} collective-permute-done((f32[512,512]{0,1:T(8,128)}, f32[512,512]{0,1:T(8,128)}, u32[]{:S(2)}, u32[]{:S(2)}) %collective-permute-start.1) | collective-permute-done | bytes 1048608 | tf_op jit(solution)/shard_map/ppermute | solution.py:13
  228.8 2.9 fusion.66
  231.7 4.3 broadcast.158.clone
  236.8 65.4 %while.66 = (s32[]{:T(128)}, bf16[512,512]{0,1:T(8,128)(2,1)}, f32[8,512,512]{1,2,0:T(8,128)}, bf16[8,2,512,512]{3,2,1,0:T(8,128)(2,1)}, f32[8,512,512]{1,2,0:T(8,128)}, /*index=5*/bf16[8,512,512]{2,1,0:T(8,128)(2,1)}, s32[]{:T(128)}) while((s32[]{:T(128)}, bf16[512,512]{0,1:T(8,128)(2,1)}, f32[8,512,512]{1,2,0:T(8,128)}, ...), condition=%wide.region_5.6_spmd, body=%wide.region_4.5_spmd.sunk | while | flops 806617088 | bytes 17302612 | solution.py:62
  240.7 2.7 fusion.149
  248.9 2.7 fusion.149
  257.0 2.7 fusion.149
  265.2 2.7 fusion.149
  273.4 2.7 fusion.149
  281.7 2.7 fusion.149
  289.9 2.7 fusion.149
  298.0 2.7 fusion.149
  302.3 4.3 broadcast.158
  306.6 67.7 %while.69 = (s32[]{:T(128)}, bf16[512,512]{0,1:T(8,128)(2,1)}, f32[8,512,512]{1,2,0:T(8,128)}, f32[8,512,512]{1,2,0:T(8,128)}, bf16[8,2,512,512]{3,2,1,0:T(8,128...) while((s32[]{:T(128)}, bf16[512,512]{0,1:T(8,128)(2,1)}, ...), condition=%wide.region_7.8_spmd.clone, body=%wide.region_6.7_spmd.clone.sunk | while | flops 807403520 | bytes 15204483 | solution.py:69
  310.3 2.5 fusion.158
  327.3 2.4 fusion.158
  344.2 2.4 fusion.158
  369.6 2.4 fusion.158
  374.3 7.7 %multiply_subtract_fusion = f32[8,512,256]{1,2,0:T(8,128)} fusion(f32[8,512,512]{1,2,0:T(8,128)} %get-tuple-element.338, f32[]{:T(128)} %bitcast.27, f32[]{:T(128)} %bitcast.8), kind=kLoop, calls=%fused_computation.67 | loop fusion | flops 3145728 | bytes 12582920 | tf_op jit(solution)/shard_map/sub | solution.py:101
  387.1 81.9 %all-reduce.6.cloned.1.call-done = f32[8,512,256]{1,2,0:T(8,128)} async-done(((f32[8,512,256]{1,2,0:T(8,128)}), f32[8,512,256]{1,2,0:T(8,128)}) %all-reduce.6.cloned.1.call-update) | async-done | bytes 4194320 | tf_op jit(solution)/shard_map/psum | solution.py:108
  472.1 9.1 %fusion.61 = f32[256,256]{0,1:T(8,128)} fusion(f32[8,512,256]{1,2,0:T(8,128)S(1)} %copy-done.5, f32[8,512,512]{1,2,0:T(8,128)} %get-tuple-element.338, f32[]{:T(128)S(6)} %add.171, f32[]{:T(128)S(6)} %sub.71, f32[]{:T(128)} %bitcast.8, bf16[1,8,512,256]{2,3,1,0:T(8,128)(2,1)S(1)} %copy-done.3), kind=kOutput, calls=%fused_computation.82 | convolution fusion | flops 3227516928 | bytes 14942220 | tf_op jit(solution)/shard_map/dot_general | solution.py:44
  481.6 129.2 %all-reduce.8.cloned.1.call-done = (f32[256,256]{0,1:T(8,128)}, f32[256,256]{0,1:T(8,128)}) async-done(((f32[256,256]{0,1:T(8,128)}, f32[256,256]{0,1:T(8,128)}), (f32[256,256]{0,1:T(8,128)}, f32[256,256]{0,1:T(8,128)})) %all-reduce.8.cloned.1.call-update) | async-done | bytes 524304 | tf_op jit(solution)/shard_map/psum | solution.py:115
  613.1 11.7 %cholesky.50 = f32[128,128]{1,0:T(8,128)S(1)} custom-call(f32[128,128]{1,0:T(8,128)S(1)} %cholesky.118), custom_call_target="Cholesky" | custom-call | tf_op jit(solution)/shard_map/jit(cholesky)/cholesky | solution.py:119
  624.8 10.0 %custom-call.17 = f32[1,128,128]{1,2,0:T(8,128)S(1)} custom-call(f32[1,128,128]{2,1,0:T(8,128)S(1)} %get-tuple-element.517), custom_call_target="InvertDiagBlocksLowerTriangular" | custom-call | tf_op jit(solution)/shard_map/jit(cholesky)/cholesky | solution.py:119
  635.3 11.7 %cholesky.105 = f32[128,128]{1,0:T(8,128)S(1)} custom-call(f32[128,128]{1,0:T(8,128)S(1)} %convolution_subtract_fusion.3), custom_call_target="Cholesky" | custom-call | tf_op jit(solution)/shard_map/jit(cholesky)/cholesky | solution.py:119
  649.8 4.0 while.67
  653.7 19.7 %custom-call.18 = f32[2,128,128]{1,2,0:T(8,128)S(1)} custom-call(f32[2,128,128]{2,1,0:T(8,128)S(1)} %get-tuple-element.354), custom_call_target="InvertDiagBlocksLowerTriangular" | custom-call | tf_op jit(solution)/shard_map/triangular_solve | solution.py:17
  (228 shorter events, 243.6 us)
Async XLA Ops:
  7.2 461.8 %all-reduce.6.cloned.1.call-start = ((), (), s32[]{:S(2)}) async-start(), calls=%async_computation | async-start | bytes 8388608 | tf_op jit(solution)/shard_map/psum | solution.py:108
  15.4 6.9 %copy-start.2 = (bf16[1,8,512,256]{2,3,1,0:T(8,128)(2,1)}, bf16[1,8,512,256]{2,3,1,0:T(8,128)(2,1)S(1)}, u32[]{:S(2)}) copy-start(bf16[1,8,512,256]{2,3,1,0:T(8,128)(2,1)S(1)} %copy.17) | copy-start | bytes 6291460
  15.9 2.1 copy-start
  18.0 4.2 copy-start.4
  168.3 28.0 %collective-permute-start = (f32[512,512]{0,1:T(8,128)S(1)}, f32[512,512]{0,1:T(8,128)S(1)}, u32[]{:S(2)}, u32[]{:S(2)}) collective-permute-start(f32[512,512]{0,1:T(8,128)S(1)} %slice_bitcast_fusion.1), channel_id=1, source_target_pairs={{1,0},{2,1},{3,2},{4,3},{5,4},{6,5},{7,6},{9,8},{10,9},{11,10},{12... | collective-permute-start | bytes 3145736 | tf_op jit(solution)/shard_map/ppermute | solution.py:13
  197.1 9.1 %copy-start.6 = (f32[1,4]{1,0:T(1,128)S(1)}, f32[1,4]{1,0:T(1,128)}, u32[]{:S(2)}) copy-start(f32[1,4]{1,0:T(1,128)} %param.23) | copy-start | bytes 52
  200.0 26.4 %collective-permute-start.1 = (f32[512,512]{0,1:T(8,128)}, f32[512,512]{0,1:T(8,128)}, u32[]{:S(2)}, u32[]{:S(2)}) collective-permute-start(f32[512,512]{0,1:T(8,128)} %convolution_bitcast_fusion.4), channel_id=1, source_target_pairs={{0,1},{1,2},{2,3},{3,4},{4,5},{5,6},{6,7},{8,9},{9,10},{10,11},{11... | collective-permute-start | bytes 3145736 | tf_op jit(solution)/shard_map/ppermute | solution.py:13
  206.1 20.3 %copy-start.1 = (f32[8,512,256]{1,2,0:T(8,128)S(1)}, f32[8,512,256]{1,2,0:T(8,128)}, u32[]{:S(2)}) copy-start(f32[8,512,256]{1,2,0:T(8,128)} %copy-done) | copy-start | bytes 12582916
  382.0 90.2 %copy-start.3 = (bf16[1,8,512,256]{2,3,1,0:T(8,128)(2,1)S(1)}, bf16[1,8,512,256]{2,3,1,0:T(8,128)(2,1)}, u32[]{:S(2)}) copy-start(bf16[1,8,512,256]{2,3,1,0:T(8,128)(2,1)} %copy-done.2) | copy-start | bytes 6291460
  382.0 228.9 %all-reduce.8.cloned.1.call-start = ((), (), s32[]{:S(2)}) async-start(), calls=%async_computation.1 | async-start | bytes 1048576 | tf_op jit(solution)/shard_map/psum | solution.py:115
  469.0 3.2 copy-start.5
Sparse Core Ops, SparseCore 0:
  382.1 86.7 all-reduce.5
  481.4 129.4 all-reduce.7
where the time goes:
time: 699 us; the launch traced here: 687 us
  waiting for transfers between devices  252 us (36%)
  other arithmetic  173 us (25%)
  local copies, waits for them, and re-layouts  128 us (18%)
  matrix products  104 us (15%)
  between operations  20.8 us (3%)
  starting transfers between devices  7.59 us (1%)
    psum x1, waiting for transfers between devices, on_device(): lax.psum((gram_part, projected_part), ('pole', 'dom'))  129 us
    dot_general x35, matrix products, complex_product(): jnp.dot(stacked, vectors.astype(jnp.bfloat16), preferred_element_type=jnp...  83.1 us
    dynamic_slice x64, local copies, waits for them, and re-layouts, partition_solve(): lax.scan(forward_step, initial, (inverse, source, previous))  82.9 us
    psum x1, waiting for transfers between devices, on_device(): summed = lax.psum(filtered_term, 'pole')  81.9 us
    dynamic_update_slice x32, other arithmetic, partition_solve(): lax.scan(forward_step, initial, (inverse, source, previous))  60.9 us
    ppermute x2, waiting for transfers between devices, shifted(): return lax.ppermute(x, axis, pairs)  41.1 us
    add x16, other arithmetic, backward_step(): partial_value + complex_product(block_inverse, real_product(couple_next,...  35.2 us
    another operation x7, other arithmetic, on_device(): factor = jnp.linalg.cholesky(gram)  34.8 us
  transfers between devices with their start and end apart: 4, of which 4 were waited for; matrix products, arithmetic and copies ran while one was open for 1% of the time, Pallas kernels for 0%

commit v1 on v0

--- a/solution.py
+++ b/solution.py
@@ -105,7 +105,10 @@
         - real_w * real_start
     )
     count = blocks // lax.axis_size("pole")
-    summed = lax.psum(filtered_term, "pole")
+    size, summed = (lax.axis_size("pole"), filtered_term)
+    for reach in [1 << k for k in range(size.bit_length() - 1)]:
+        pairs_2 = [(i_2, i_2 ^ reach) for i_2 in range(size)]
+        summed = summed + lax.ppermute(summed, "pole", pairs_2)
     offset = lax.axis_index("pole") * count
     own_rows = lax.dynamic_slice_in_dim(summed, offset, count, 0).reshape(count * B, M)
     gram_part = inner_products(own_rows, own_rows)

time: 699 us -> 721 us (1.031)
  waiting for transfers between devices: 252 us -> 265 us
  other arithmetic: 173 us -> 182 us
    ppermute x0 -> x2, waiting for transfers between devices: none -> 93.8 us  [on_device(): summed = summed + lax.ppermute(summed, 'pole', pairs_2)]
    psum x1 -> x0, waiting for transfers between devices: 81.9 us -> none  [on_device(): summed = lax.psum(filtered_term, 'pole')]
    add x0 -> x2, other arithmetic: none -> 9.29 us  [on_device(): summed = summed + lax.ppermute(summed, 'pole', pairs_2)]
  transfers between devices with their start and end apart: 4 -> 5, of which waited for: 4 -> 5; matrix products, arithmetic and copies ran while one was open for 1% -> 1% of each run, Pallas kernels for 0% -> 0%
where the time goes in v1:
time: 721 us; the launch traced here: 709 us
  waiting for transfers between devices  265 us (37%)
  other arithmetic  182 us (25%)
  local copies, waits for them, and re-layouts  127 us (18%)
  matrix products  104 us (14%)
  between operations  21 us (3%)
  starting transfers between devices  9.01 us (1%)
    psum x1, waiting for transfers between devices, on_device(): lax.psum((gram_part, projected_part), ('pole', 'dom'))  130 us
    ppermute x2, waiting for transfers between devices, on_device(): summed = summed + lax.ppermute(summed, 'pole', pairs_2)  93.8 us
    dot_general x35, matrix products, complex_product(): jnp.dot(stacked, vectors.astype(jnp.bfloat16), preferred_element_type=jnp...  83.1 us
    dynamic_slice x64, local copies, waits for them, and re-layouts, partition_solve(): lax.scan(forward_step, initial, (inverse, source, previous))  82.9 us
    dynamic_update_slice x32, other arithmetic, partition_solve(): lax.scan(forward_step, initial, (inverse, source, previous))  60.9 us
    ppermute x2, waiting for transfers between devices, shifted(): return lax.ppermute(x, axis, pairs)  41.1 us
    add x16, other arithmetic, backward_step(): partial_value + complex_product(block_inverse, real_product(couple_next,...  35.4 us
    another operation x7, other arithmetic, on_device(): factor = jnp.linalg.cholesky(gram)  34.8 us
  transfers between devices with their start and end apart: 5, of which 5 were waited for; matrix products, arithmetic and copies ran while one was open for 1% of the time, Pallas kernels for 0%

profile of v1, /device:TPU:0, one launch (start us, length us, event | category | flops | bytes accessed | tf_op | source)
XLA Modules:
  0.0 709.0 jit_solution(16176408510340880278)
XLA Ops:
  7.2 4.2 slice_bitcast_fusion
  12.5 2.9 copy.17
  18.0 4.2 concatenate.76
  24.6 4.3 broadcast.158.clone.2
  29.8 65.2 %while.65 = (s32[]{:T(128)}, bf16[512,512]{0,1:T(8,128)(2,1)}, f32[8,512,512]{1,2,0:T(8,128)}, bf16[8,2,512,512]{3,2,1,0:T(8,128)(2,1)}, f32[8,512,512]{1,2,0:T(8,128)}, /*index=5*/bf16[8,512,512]{2,1,0:T(8,128)(2,1)}, s32[]{:T(128)}) while((s32[]{:T(128)}, bf16[512,512]{0,1:T(8,128)(2,1)}, f32[8,512,512]{1,2,0:T(8,128)}, ...), condition=%wide.region_1.2_spmd, body=%wide.region_0.1_spmd.sunk | while | flops 806617088 | bytes 17302612 | solution.py:62
  33.7 2.7 fusion.146
  41.8 2.7 fusion.146
  49.9 2.7 fusion.146
  58.1 2.7 fusion.146
  66.3 2.7 fusion.146
  74.5 2.7 fusion.146
  82.6 2.7 fusion.146
  90.8 2.7 fusion.146
  95.0 4.3 broadcast.158.clone.1
  99.3 67.8 %while.68 = (s32[]{:T(128)}, bf16[512,512]{0,1:T(8,128)(2,1)}, f32[8,512,512]{1,2,0:T(8,128)}, f32[8,512,512]{1,2,0:T(8,128)}, bf16[8,2,512,512]{3,2,1,0:T(8,128...) while((s32[]{:T(128)}, bf16[512,512]{0,1:T(8,128)(2,1)}, ...), condition=%wide.region_3.4_spmd.clone, body=%wide.region_2.3_spmd.clone.sunk | while | flops 807403520 | bytes 15204483 | solution.py:69
  103.0 2.5 fusion.155
  120.1 2.4 fusion.155
  174.0 22.5 %collective-permute-done = f32[512,512]{0,1:T(8,128)S(1)} collective-permute-done((f32[512,512]{0,1:T(8,128)S(1)}, f32[512,512]{0,1:T(8,128)S(1)}, u32[]{:S(2)}, u32[]{:S(2)}) %collective-permute-start) | collective-permute-done | bytes 1048608 | tf_op jit(solution)/shard_map/ppermute | solution.py:13
  197.7 2.5 convolution_bitcast_fusion.4
  200.2 6.1 collective-permute-start.1
  207.9 18.7 %collective-permute-done.1 = f32[512,512]{0,1:T(8,128)} collective-permute-done((f32[512,512]{0,1:T(8,128)}, f32[512,512]{0,1:T(8,128)}, u32[]{:S(2)}, u32[]{:S(2)}) %collective-permute-start.1) | collective-permute-done | bytes 1048608 | tf_op jit(solution)/shard_map/ppermute | solution.py:13
  228.9 2.9 fusion.66
  231.8 4.3 broadcast.158.clone
  237.0 65.5 %while.66 = (s32[]{:T(128)}, bf16[512,512]{0,1:T(8,128)(2,1)}, f32[8,512,512]{1,2,0:T(8,128)}, bf16[8,2,512,512]{3,2,1,0:T(8,128)(2,1)}, f32[8,512,512]{1,2,0:T(8,128)}, /*index=5*/bf16[8,512,512]{2,1,0:T(8,128)(2,1)}, s32[]{:T(128)}) while((s32[]{:T(128)}, bf16[512,512]{0,1:T(8,128)(2,1)}, f32[8,512,512]{1,2,0:T(8,128)}, ...), condition=%wide.region_5.6_spmd, body=%wide.region_4.5_spmd.sunk | while | flops 806617088 | bytes 17302612 | solution.py:62
  240.9 2.7 fusion.150
  249.1 2.7 fusion.150
  257.2 2.7 fusion.150
  265.4 2.7 fusion.150
  273.6 2.7 fusion.150
  281.9 2.7 fusion.150
  290.1 2.7 fusion.150
  298.2 2.7 fusion.150
  302.5 4.3 broadcast.158
  306.9 67.9 %while.69 = (s32[]{:T(128)}, bf16[512,512]{0,1:T(8,128)(2,1)}, f32[8,512,512]{1,2,0:T(8,128)}, f32[8,512,512]{1,2,0:T(8,128)}, bf16[8,2,512,512]{3,2,1,0:T(8,128...) while((s32[]{:T(128)}, bf16[512,512]{0,1:T(8,128)(2,1)}, ...), condition=%wide.region_7.8_spmd.clone, body=%wide.region_6.7_spmd.clone.sunk | while | flops 807403520 | bytes 15204483 | solution.py:69
  310.6 2.5 fusion.159
  369.9 2.4 fusion.159
  374.8 6.3 multiply_subtract_fusion
  381.1 7.1 %collective-permute-done.2 = f32[8,512,256]{1,2,0:T(8,128)S(1)} collective-permute-done((f32[8,512,256]{1,2,0:T(8,128)S(1)}, f32[8,512,256]{1,2,0:T(8,128)S(1)}, u32[]{:S(2)}, u32[]{:S(2)}) %collective-permute-start.2) | collective-permute-done | bytes 4194336 | tf_op jit(solution)/shard_map/ppermute | solution.py:111
  388.3 4.8 fusion.125
  399.4 86.6 %collective-permute-done.3 = f32[8,512,256]{1,2,0:T(8,128)} collective-permute-done((f32[8,512,256]{1,2,0:T(8,128)}, f32[8,512,256]{1,2,0:T(8,128)}, u32[]{:S(2)}, u32[]{:S(2)}) %collective-permute-start.3) | collective-permute-done | bytes 4194336 | tf_op jit(solution)/shard_map/ppermute | solution.py:111
  486.0 4.5 add.174
  492.3 9.1 %fusion.61 = f32[256,256]{0,1:T(8,128)} fusion(f32[8,512,256]{1,2,0:T(8,128)S(1)} %add.174, f32[8,512,512]{1,2,0:T(8,128)} %get-tuple-element.338, f32[]{:T(128)S(6)} %add.177, f32[]{:T(128)S(6)} %sub.71, f32[]{:T(128)} %bitcast.8, bf16[1,8,512,256]{2,3,1,0:T(8,128)(2,1)S(1)} %copy-done.4), kind=kOutput, calls=%fused_computation.81 | convolution fusion | flops 3227516928 | bytes 14942220 | tf_op jit(solution)/shard_map/dot_general | solution.py:44
  501.8 130.4 %all-reduce.5.cloned.1.call-done = (f32[256,256]{0,1:T(8,128)}, f32[256,256]{0,1:T(8,128)}) async-done(((f32[256,256]{0,1:T(8,128)}, f32[256,256]{0,1:T(8,128)}), (f32[256,256]{0,1:T(8,128)}, f32[256,256]{0,1:T(8,128)})) %all-reduce.5.cloned.1.call-update) | async-done | bytes 524304 | tf_op jit(solution)/shard_map/psum | solution.py:118
  634.4 11.9 %cholesky.50 = f32[128,128]{1,0:T(8,128)S(1)} custom-call(f32[128,128]{1,0:T(8,128)S(1)} %cholesky.118), custom_call_target="Cholesky" | custom-call | tf_op jit(solution)/shard_map/jit(cholesky)/cholesky | solution.py:122
  646.4 9.8 %custom-call.17 = f32[1,128,128]{1,2,0:T(8,128)S(1)} custom-call(f32[1,128,128]{2,1,0:T(8,128)S(1)} %get-tuple-element.517), custom_call_target="InvertDiagBlocksLowerTriangular" | custom-call | tf_op jit(solution)/shard_map/jit(cholesky)/cholesky | solution.py:122
  656.7 11.7 %cholesky.105 = f32[128,128]{1,0:T(8,128)S(1)} custom-call(f32[128,128]{1,0:T(8,128)S(1)} %convolution_subtract_fusion.1), custom_call_target="Cholesky" | custom-call | tf_op jit(solution)/shard_map/jit(cholesky)/cholesky | solution.py:122
  671.1 4.0 while.67
  675.1 19.9 %custom-call.18 = f32[2,128,128]{1,2,0:T(8,128)S(1)} custom-call(f32[2,128,128]{2,1,0:T(8,128)S(1)} %get-tuple-element.354), custom_call_target="InvertDiagBlocksLowerTriangular" | custom-call | tf_op jit(solution)/shard_map/triangular_solve | solution.py:17
  (231 shorter events, 251.1 us)
Async XLA Ops:
  7.2 625.1 %all-reduce.5.cloned.1.call-start = ((), (), s32[]{:S(2)}) async-start(), calls=%async_computation | async-start | bytes 1048576 | tf_op jit(solution)/shard_map/psum | solution.py:118
  15.4 6.9 copy-start.3
  16.0 2.1 copy-start.1
  18.0 4.3 copy-start.5
  168.4 28.0 %collective-permute-start = (f32[512,512]{0,1:T(8,128)S(1)}, f32[512,512]{0,1:T(8,128)S(1)}, u32[]{:S(2)}, u32[]{:S(2)}) collective-permute-start(f32[512,512]{0,1:T(8,128)S(1)} %slice_bitcast_fusion.1), channel_id=1, source_target_pairs={{1,0},{2,1},{3,2},{4,3},{5,4},{6,5},{7,6},{9,8},{10,9},{11,10},{12... | collective-permute-start | bytes 3145736 | tf_op jit(solution)/shard_map/ppermute | solution.py:13
  197.2 9.1 %copy-start.6 = (f32[1,4]{1,0:T(1,128)S(1)}, f32[1,4]{1,0:T(1,128)}, u32[]{:S(2)}) copy-start(f32[1,4]{1,0:T(1,128)} %param.23) | copy-start | bytes 52
  200.2 26.4 %collective-permute-start.1 = (f32[512,512]{0,1:T(8,128)}, f32[512,512]{0,1:T(8,128)}, u32[]{:S(2)}, u32[]{:S(2)}) collective-permute-start(f32[512,512]{0,1:T(8,128)} %convolution_bitcast_fusion.4), channel_id=1, source_target_pairs={{0,1},{1,2},{2,3},{3,4},{4,5},{5,6},{6,7},{8,9},{9,10},{10,11},{11... | collective-permute-start | bytes 3145736 | tf_op jit(solution)/shard_map/ppermute | solution.py:13
  206.3 20.3 %copy-start.2 = (f32[8,512,256]{1,2,0:T(8,128)S(1)}, f32[8,512,256]{1,2,0:T(8,128)}, u32[]{:S(2)}) copy-start(f32[8,512,256]{1,2,0:T(8,128)} %copy-done.1) | copy-start | bytes 12582916
  374.7 13.5 %copy-start = (f32[8,512,512]{1,2,0:T(8,128)S(1)}, f32[8,512,512]{1,2,0:T(8,128)}, u32[]{:S(2)}) copy-start(f32[8,512,512]{1,2,0:T(8,128)} %get-tuple-element.338) | copy-start | bytes 25165828
  381.0 7.2 %collective-permute-start.2 = (f32[8,512,256]{1,2,0:T(8,128)S(1)}, f32[8,512,256]{1,2,0:T(8,128)S(1)}, u32[]{:S(2)}, u32[]{:S(2)}) collective-permute-start(f32[8,512,256]{1,2,0:T(8,128)S(1)} %multiply_subtract_fusion), channel_id=1, source_target_pairs={{0,8},{8,0},{16,24},{24,16},{1,9},{9,1},{17,25},{25,17},{2,10},{10... | collective-permute-start | bytes 12582920 | tf_op jit(solution)/shard_map/ppermute | solution.py:111
  393.1 92.9 %collective-permute-start.3 = (f32[8,512,256]{1,2,0:T(8,128)}, f32[8,512,256]{1,2,0:T(8,128)}, u32[]{:S(2)}, u32[]{:S(2)}) collective-permute-start(f32[8,512,256]{1,2,0:T(8,128)} %fusion.125), channel_id=1, source_target_pairs={{0,16},{8,24},{16,0},{24,8},{1,17},{9,25},{17,1},{25,9},{2,18},{10... | collective-permute-start | bytes 12582920 | tf_op jit(solution)/shard_map/ppermute | solution.py:111
  490.5 1.8 copy-start.4
Sparse Core Ops, SparseCore 0:
  501.5 130.6 all-reduce.4
